TPU v7x, 512 devices: a whole 4x8x8 slice. The times are simulated.
512 devices in a mesh: kgrp: 128 (over y, x, z_hi), img: 4 (over z_lo, core).
Axes of the slice: x: 4, y: 8, z: 8 (z_hi: 4, z_lo: 2; z = z_hi * 2 + z_lo), core: 2. Of those that a mesh axis runs over, the one named last changes fastest.
Arguments:
- vectors: float32 [2, 16, 16384], P(None, 'img', 'kgrp'), may hold values from -6 to 6
- conduction: bfloat16 [256, 2, 8, 4, 4096], P('kgrp', None, None, 'img'), may hold values from -6 to 6
- valence: bfloat16 [256, 2, 8, 4, 4096], P('kgrp', None, None, 'img'), may hold values from -6 to 6
- hole_point: int32 [1], replicated, may hold values from 0 to 16383
- kpoint_grid: int32 [3, 256], replicated, may hold values from 0 to 11
- image_cells: int32 [3, 512], replicated, may hold values from -6 to 6
Outputs:
- psi_real: float32 [16, 4, 4096, 512], P(None, 'img', 'kgrp')
- psi_imag: float32 [16, 4, 4096, 512], P(None, 'img', 'kgrp')
All inputs are finite; a program needn't handle non-finite values.
Results may differ from a plain program's by a relative error of at most 0.0043.
Values may be sent and summed in bfloat16 or wider, within the bound.
A program may use at most 64 MiB of HBM per device.

v0:
```python
import jax
import jax.numpy as jnp
import numpy as np
from jax import lax
from jax.sharding import PartitionSpec as P

NV = 8
NC = 8
cosine_levels = np.cos(2.0 * np.pi * np.arange(12) / 12.0)
sine_levels = np.sin(2.0 * np.pi * np.arange(12) / 12.0)


def phase_table(kpoint_grid, image_cells):
    turn_count = kpoint_grid[0][:, None] * image_cells[0][None, :]
    turn_count = turn_count + kpoint_grid[1][:, None] * image_cells[1][None, :]
    turn_count = turn_count + kpoint_grid[2][:, None] * image_cells[2][None, :]
    turn_count = jnp.mod(turn_count, 12)
    cosine = jnp.zeros(turn_count.shape, jnp.float32)
    sine_part = jnp.zeros(turn_count.shape, jnp.float32)
    for level_index in range(12):
        matches = turn_count == level_index
        cosine = jnp.where(matches, jnp.float32(cosine_levels[level_index]), cosine)
        sine_part = jnp.where(matches, jnp.float32(sine_levels[level_index]), sine_part)
    upper_half = jnp.stack([cosine, sine_part], 1)
    lower_half = jnp.stack([-sine_part, cosine], 1)
    return jnp.stack([upper_half, lower_half], 0).astype(jnp.bfloat16)


def hole_weights(amplitudes, hole_values):
    norm_factor = (NV * NC) ** (-0.5)
    real_amplitude = amplitudes[0]
    imaginary_amplitude = amplitudes[1]
    real_hole = hole_values[:, 0]
    imaginary_hole = hole_values[:, 1]
    highest = lax.Precision.HIGHEST
    weight_real = jnp.einsum("skvc,kv->ksc", real_amplitude, real_hole, precision=highest)
    weight_real = weight_real + jnp.einsum(
        "skvc,kv->ksc", imaginary_amplitude, imaginary_hole, precision=highest
    )
    weight_imaginary = jnp.einsum("skvc,kv->ksc", imaginary_amplitude, real_hole, precision=highest)
    weight_imaginary = weight_imaginary - jnp.einsum(
        "skvc,kv->ksc", real_amplitude, imaginary_hole, precision=highest
    )
    return jnp.stack([weight_real * norm_factor, weight_imaginary * norm_factor], 1).astype(
        jnp.bfloat16
    )


def mixing(weights):
    weight_real = weights[:, 0]
    weight_imaginary = weights[:, 1]
    first_row = jnp.stack([weight_real, -weight_imaginary], 2)
    second_row = jnp.stack([weight_imaginary, weight_real], 2)
    return jnp.stack([first_row, second_row], 1)


def shards(vectors, conduction, valence, hole_point, kpoint_grid, image_cells):
    group_size = lax.axis_size("kgrp")
    local_k = conduction.shape[0]
    slab_width = conduction.shape[4]
    own_excitons = vectors.shape[1]
    blocks = vectors.shape[2] // group_size
    columns = vectors.reshape(2, own_excitons, group_size, blocks)
    owned_columns = lax.all_to_all(columns, "kgrp", split_axis=2, concat_axis=2, tiled=True)
    owned_columns = owned_columns.reshape(2, own_excitons, local_k, NV, NC)
    hole_offset = hole_point[0] % slab_width
    hole_slab = hole_point[0] // slab_width
    present = (lax.axis_index("img") == hole_slab).astype(jnp.float32)
    picked = (
        lax.dynamic_slice_in_dim(valence[:, :, :, 0, :], hole_offset, 1, 3)[..., 0].astype(
            jnp.float32
        )
        * present
    )
    hole_values = lax.psum(picked, "img")
    all_columns = lax.all_gather(owned_columns, "img", axis=1, tiled=True)
    weights = hole_weights(all_columns, hole_values)
    phases = phase_table(kpoint_grid, image_cells)
    products = jnp.einsum(
        "kasbc,kbcp->sakp",
        mixing(weights),
        conduction[:, :, :, 0, :],
        preferred_element_type=jnp.float32,
    ).astype(jnp.bfloat16)
    summed = jnp.einsum(
        "sakp,akbn->spbn",
        lax.all_to_all(products, "kgrp", split_axis=3, concat_axis=2, tiled=True),
        phases,
        preferred_element_type=jnp.float32,
    )
    normal_scale = (2 * kpoint_grid.shape[1]) ** (-0.5)
    summed = summed * normal_scale
    return (summed[:, None, :, 0, :], summed[:, None, :, 1, :])


def solution(mesh):
    placed = (
        P(None, "img", "kgrp"),
        P("kgrp", None, None, "img", None),
        P("kgrp", None, None, "img", None),
        P(),
        P(),
        P(),
    )
    return jax.shard_map(
        shards,
        mesh=mesh,
        in_specs=placed,
        out_specs=(P(None, "img", "kgrp", None), P(None, "img", "kgrp", None)),
        check_vma=False,
    )
```

profile of v0, /device:TPU:8, one launch (start us, length us, event | category | flops | bytes accessed | tf_op | source)
XLA Modules:
  0.0 111.9 jit_solution(5236022632202495821)
XLA Ops:
  0.6 0.0 copy-start
  0.6 1.5 %copy.29 = f32[2,4,128]{1,0,2:T(2,128)} copy(f32[2,4,128]{2,1,0:T(4,128)} %param.6) | data formatting | bytes 8192 | tf_op args[0]
  2.2 19.8 %all-to-all-start = ((f32[2,4,128,1]{1,0,3,2:T(2,128)}), f32[2,4,128,1]{1,0,3,2:T(2,128)S(1)}, u32[]{:S(2)}, u32[]{:S(2)}) async-start(f32[2,4,128,1]{1,0,3,2:T(2,128)} %bitcast.4), calls=%async_computation | async-start | bytes 262144 | tf_op jit(solution)/shard_map/all_to_all | solution.py:64
  22.7 0.9 multiply_reduce_fusion
  23.5 6.3 %psum.7 = f32[2,2,8]{2,1,0:T(2,128)S(1)} all-reduce(f32[2,2,8]{2,1,0:T(2,128)S(1)} %multiply_reduce_fusion), channel_id=1, replica_groups=mesh['kgrp'=128,'img'=4] {'img'}, use_global_device_ids=true, to_apply=%region_0.1 | all-reduce | flops 32 | bytes 256 | tf_op jit(solution)/shard_map/psum | solution.py:75
  29.9 6.6 %all-to-all-done = f32[2,4,128,1]{1,0,3,2:T(2,128)S(1)} async-done(((f32[2,4,128,1]{1,0,3,2:T(2,128)}), f32[2,4,128,1]{1,0,3,2:T(2,128)S(1)}, u32[]{:S(2)}, u32[]{:S(2)}) %all-to-all-start) | async-done | bytes 4128 | tf_op jit(solution)/shard_map/all_to_all | solution.py:64
  36.5 0.3 copy.30
  36.8 5.8 %all_gather.3 = f32[2,16,2,8,8]{4,3,2,0,1:T(8,128)S(1)} all-gather(f32[2,4,2,8,8]{4,3,2,0,1:T(8,128)S(1)} %copy.30), channel_id=1, replica_groups=mesh['kgrp'=128,'img'=4] {'img'}, dimensions={1}, use_global_device_ids=true | all-gather | bytes 20480 | tf_op jit(solution)/shard_map/all_gather | solution.py:76
  42.6 0.3 fusion.15
  42.8 0.3 fusion.13
  43.1 0.3 fusion.19
  43.4 0.3 fusion.17
  43.6 0.1 copy.41
  43.7 0.1 copy.44
  43.8 0.1 copy.45
  43.8 0.1 copy.46
  43.9 0.0 copy-done
  43.9 0.3 fusion.1
  44.3 7.1 %copy.32 = bf16[16,2,2,4096]{0,1,2,3:T(2,128)(2,1)} copy(bf16[16,2,2,4096]{3,0,1,2:T(8,128)(2,1)S(1)} %fusion.1) | data formatting | bytes 1048576 | tf_op jit(solution)/shard_map/convert_element_type | solution.py:84
  51.4 0.0 copy-start.2
  51.4 0.0 copy-start.1
  51.4 12.9 %reshape.653 = bf16[128,2,1024]{2,1,0:T(2,128)(2,1)} reshape(bf16[4096,2,2,16]{3,2,1,0:T(2,128)(2,1)} %bitcast.114) | data formatting | bytes 1048576
  64.3 9.2 %all-to-all-start.1 = ((bf16[128,2,1024]{2,1,0:T(2,128)(2,1)}), bf16[128,2,1024]{2,1,0:T(2,128)(2,1)S(1)}, u32[]{:S(2)}, u32[]{:S(2)}) async-start(bf16[128,2,1024]{2,1,0:T(2,128)(2,1)} %reshape.653), calls=%async_computation.1 | async-start | bytes 1048576 | tf_op jit(solution)/shard_map/all_to_all | solution.py:87
  73.5 0.0 copy-done.2
  73.6 0.0 copy-done.1
  73.6 1.1 fusion.12
  74.6 0.1 maximum_bitcast_fusion.2
  74.7 22.0 %all-to-all-done.1 = bf16[128,2,1024]{2,1,0:T(2,128)(2,1)S(1)} async-done(((bf16[128,2,1024]{2,1,0:T(2,128)(2,1)}), bf16[128,2,1024]{2,1,0:T(2,128)(2,1)S(1)}, u32[]{:S(2)}, u32[]{:S(2)}) %all-to-all-start.1) | async-done | bytes 524320 | tf_op jit(solution)/shard_map/all_to_all | solution.py:87
  96.8 4.1 %reshape.654 = bf16[4096,2,2,16]{3,2,1,0:T(2,128)(2,1)} reshape(bf16[128,2,1024]{2,1,0:T(2,128)(2,1)S(1)} %all-to-all-done.1) | data formatting | bytes 1048576
  100.9 8.6 %copy.52 = bf16[16,2,2,128,32]{4,0,2,3,1:T(8,128)(2,1)S(1)} copy(bf16[16,2,2,128,32]{0,1,2,4,3:T(2,128)(2,1)} %bitcast.115) | data formatting | bytes 1048576 | tf_op jit(solution)/shard_map/all_to_all | solution.py:87
  109.5 1.0 bitcast_multiply_fusion
  110.4 1.5 %slice_bitcast_fusion = (f32[16,1,32,512]{3,2,1,0:T(8,128)}, f32[16,1,32,512]{3,2,1,0:T(8,128)}) fusion(f32[16,32,2,512]{3,1,2,0:T(8,128)S(1)} %bitcast_multiply_fusion), kind=kLoop, calls=%fused_computation.6 | loop fusion | bytes 4194304
  (6 shorter events, 0.1 us)
Async XLA Ops:
  0.6 43.3 %copy-start = (bf16[2,2,8,1,4096]{4,2,3,1,0:T(8,128)(2,1)S(1)}, bf16[2,2,8,1,4096]{4,2,3,1,0:T(8,128)(2,1)}, u32[]{:S(2)}) copy-start(bf16[2,2,8,1,4096]{4,2,3,1,0:T(8,128)(2,1)} %param.7) | copy-start | bytes 786436
  2.2 34.3 %all-to-all-start = ((f32[2,4,128,1]{1,0,3,2:T(2,128)}), f32[2,4,128,1]{1,0,3,2:T(2,128)S(1)}, u32[]{:S(2)}, u32[]{:S(2)}) async-start(f32[2,4,128,1]{1,0,3,2:T(2,128)} %bitcast.4), calls=%async_computation | async-start | bytes 262144 | tf_op jit(solution)/shard_map/all_to_all | solution.py:64
  51.4 22.1 %copy-start.2 = (s32[3,256]{1,0:T(4,128)S(1)}, s32[3,256]{1,0:T(4,128)}, u32[]{:S(2)}) copy-start(s32[3,256]{1,0:T(4,128)} %param.10) | copy-start | bytes 9220
  51.4 22.1 %copy-start.1 = (s32[3,512]{1,0:T(4,128)S(1)}, s32[3,512]{1,0:T(4,128)}, u32[]{:S(2)}) copy-start(s32[3,512]{1,0:T(4,128)} %param.11) | copy-start | bytes 18436
  64.3 32.4 %all-to-all-start.1 = ((bf16[128,2,1024]{2,1,0:T(2,128)(2,1)}), bf16[128,2,1024]{2,1,0:T(2,128)(2,1)S(1)}, u32[]{:S(2)}, u32[]{:S(2)}) async-start(bf16[128,2,1024]{2,1,0:T(2,128)(2,1)} %reshape.653), calls=%async_computation.1 | async-start | bytes 1048576 | tf_op jit(solution)/shard_map/all_to_all | solution.py:87
where the time goes:
time: 112 us
  local copies, waits for them, and re-layouts  36.4 us (32%)
  starting transfers between devices  29 us (26%)
  waiting for transfers between devices  28.6 us (26%)
  blocking collectives  12.1 us (11%)
  matrix products  2.31 us (2%)
  other arithmetic  2.02 us (2%)
  between operations  1.47 us (1%)
    all_to_all x1, waiting for transfers between devices, shards(): lax.all_to_all(products, 'kgrp', split_axis=3, concat_axis=2, tiled=True)  22 us
    unnamed x10, local copies, waits for them, and re-layouts  20.1 us
    all_to_all x1, starting transfers between devices, shards(): lax.all_to_all(columns, 'kgrp', split_axis=2, concat_axis=2, tiled=True)  19.8 us
    all_to_all x1, starting transfers between devices, shards(): lax.all_to_all(products, 'kgrp', split_axis=3, concat_axis=2, tiled=True)  9.2 us
    all_to_all x1, local copies, waits for them, and re-layouts, shards(): lax.all_to_all(products, 'kgrp', split_axis=3, concat_axis=2, tiled=True)  8.56 us
    convert_element_type x1, local copies, waits for them, and re-layouts, shards(): products = jnp.einsum('kasbc,kbcp->sakp', mixing(weights), conduction[:,...  7.13 us
    all_to_all x1, waiting for transfers between devices, shards(): lax.all_to_all(columns, 'kgrp', split_axis=2, concat_axis=2, tiled=True)  6.61 us
    psum x1, blocking collectives, shards(): hole_values = lax.psum(picked, 'img')  6.33 us
  transfers between devices with their start and end apart: 2, of which 2 were waited for; matrix products, arithmetic and copies ran while one was open for 2% of the time, Pallas kernels for 0%

commit v1 on v0

--- a/solution.py
+++ b/solution.py
@@ -73,7 +73,7 @@
         * present
     )
     hole_values = lax.psum(picked, "img")
-    all_columns = lax.all_gather(owned_columns, "img", axis=1, tiled=True)
+    all_columns = jnp.concatenate(lax.all_gather(owned_columns, "img"), axis=1)
     weights = hole_weights(all_columns, hole_values)
     phases = phase_table(kpoint_grid, image_cells)
     products = jnp.einsum(

time: 112 us -> 112 us (level)
  no operation moved by 1% of the time
where the time goes in v1:
time: 112 us
  local copies, waits for them, and re-layouts  36.4 us (32%)
  starting transfers between devices  29 us (26%)
  waiting for transfers between devices  28.6 us (26%)
  blocking collectives  12.1 us (11%)
  matrix products  2.3 us (2%)
  other arithmetic  2.02 us (2%)
  between operations  1.47 us (1%)
    all_to_all x1, waiting for transfers between devices, shards(): lax.all_to_all(products, 'kgrp', split_axis=3, concat_axis=2, tiled=True)  22 us
    unnamed x10, local copies, waits for them, and re-layouts  20.1 us
    all_to_all x1, starting transfers between devices, shards(): lax.all_to_all(columns, 'kgrp', split_axis=2, concat_axis=2, tiled=True)  19.8 us
    all_to_all x1, starting transfers between devices, shards(): lax.all_to_all(products, 'kgrp', split_axis=3, concat_axis=2, tiled=True)  9.19 us
    all_to_all x1, local copies, waits for them, and re-layouts, shards(): lax.all_to_all(products, 'kgrp', split_axis=3, concat_axis=2, tiled=True)  8.56 us
    convert_element_type x1, local copies, waits for them, and re-layouts, shards(): products = jnp.einsum('kasbc,kbcp->sakp', mixing(weights), conduction[:,...  7.13 us
    all_to_all x1, waiting for transfers between devices, shards(): lax.all_to_all(columns, 'kgrp', split_axis=2, concat_axis=2, tiled=True)  6.61 us
    psum x1, blocking collectives, shards(): hole_values = lax.psum(picked, 'img')  6.33 us
  transfers between devices with their start and end apart: 2, of which 2 were waited for; matrix products, arithmetic and copies ran while one was open for 2% of the time, Pallas kernels for 0%

profile of v1, /device:TPU:8, one launch (start us, length us, event | category | flops | bytes accessed | tf_op | source)
XLA Modules:
  0.0 111.9 jit_solution(3656365119575708401)
XLA Ops:
  0.6 0.0 copy-start
  0.6 1.5 %copy.20 = f32[2,4,128]{1,0,2:T(2,128)} copy(f32[2,4,128]{2,1,0:T(4,128)} %param.6) | data formatting | bytes 8192 | tf_op args[0]
  2.2 19.8 %all-to-all-start = ((f32[2,4,128,1]{1,0,3,2:T(2,128)}), f32[2,4,128,1]{1,0,3,2:T(2,128)S(1)}, u32[]{:S(2)}, u32[]{:S(2)}) async-start(f32[2,4,128,1]{1,0,3,2:T(2,128)} %bitcast.4), calls=%async_computation | async-start | bytes 262144 | tf_op jit(solution)/shard_map/all_to_all | solution.py:64
  22.7 0.9 multiply_reduce_fusion
  23.5 6.3 %psum.7 = f32[2,2,8]{2,1,0:T(2,128)S(1)} all-reduce(f32[2,2,8]{2,1,0:T(2,128)S(1)} %multiply_reduce_fusion), channel_id=1, replica_groups=mesh['kgrp'=128,'img'=4] {'img'}, use_global_device_ids=true, to_apply=%region_0.1 | all-reduce | flops 32 | bytes 256 | tf_op jit(solution)/shard_map/psum | solution.py:75
  29.9 6.6 %all-to-all-done = f32[2,4,128,1]{1,0,3,2:T(2,128)S(1)} async-done(((f32[2,4,128,1]{1,0,3,2:T(2,128)}), f32[2,4,128,1]{1,0,3,2:T(2,128)S(1)}, u32[]{:S(2)}, u32[]{:S(2)}) %all-to-all-start) | async-done | bytes 4128 | tf_op jit(solution)/shard_map/all_to_all | solution.py:64
  36.5 0.3 copy.21
  36.8 5.8 %all_gather.3 = f32[4,2,4,2,8,8]{5,4,3,2,1,0:T(8,128)S(1)} all-gather(f32[1,2,4,2,8,8]{5,4,3,2,1,0:T(8,128)S(1)} %copy.21), channel_id=1, replica_groups=mesh['kgrp'=128,'img'=4] {'img'}, dimensions={0}, use_global_device_ids=true | all-gather | bytes 20480 | tf_op jit(solution)/shard_map/all_gather | solution.py:76
  42.6 0.3 fusion.15
  42.8 0.3 fusion.13
  43.1 0.3 fusion.19
  43.3 0.3 fusion.17
  43.6 0.1 copy.32
  43.7 0.1 copy.35
  43.7 0.1 copy.36
  43.8 0.1 copy.37
  43.9 0.0 copy-done
  43.9 0.3 fusion.1
  44.3 7.1 %copy.23 = bf16[16,2,2,4096]{0,1,2,3:T(2,128)(2,1)} copy(bf16[16,2,2,4096]{3,0,1,2:T(8,128)(2,1)S(1)} %fusion.1) | data formatting | bytes 1048576 | tf_op jit(solution)/shard_map/convert_element_type | solution.py:84
  51.4 0.0 copy-start.2
  51.4 0.0 copy-start.1
  51.4 12.9 %reshape.658 = bf16[128,2,1024]{2,1,0:T(2,128)(2,1)} reshape(bf16[4096,2,2,16]{3,2,1,0:T(2,128)(2,1)} %bitcast.113) | data formatting | bytes 1048576
  64.3 9.2 %all-to-all-start.1 = ((bf16[128,2,1024]{2,1,0:T(2,128)(2,1)}), bf16[128,2,1024]{2,1,0:T(2,128)(2,1)S(1)}, u32[]{:S(2)}, u32[]{:S(2)}) async-start(bf16[128,2,1024]{2,1,0:T(2,128)(2,1)} %reshape.658), calls=%async_computation.1 | async-start | bytes 1048576 | tf_op jit(solution)/shard_map/all_to_all | solution.py:87
  73.5 0.0 copy-done.2
  73.5 0.0 copy-done.1
  73.6 1.1 fusion.12
  74.6 0.1 maximum_bitcast_fusion.2
  74.7 22.0 %all-to-all-done.1 = bf16[128,2,1024]{2,1,0:T(2,128)(2,1)S(1)} async-done(((bf16[128,2,1024]{2,1,0:T(2,128)(2,1)}), bf16[128,2,1024]{2,1,0:T(2,128)(2,1)S(1)}, u32[]{:S(2)}, u32[]{:S(2)}) %all-to-all-start.1) | async-done | bytes 524320 | tf_op jit(solution)/shard_map/all_to_all | solution.py:87
  96.8 4.1 %reshape.659 = bf16[4096,2,2,16]{3,2,1,0:T(2,128)(2,1)} reshape(bf16[128,2,1024]{2,1,0:T(2,128)(2,1)S(1)} %all-to-all-done.1) | data formatting | bytes 1048576
  100.9 8.6 %copy.43 = bf16[16,2,2,128,32]{4,0,2,3,1:T(8,128)(2,1)S(1)} copy(bf16[16,2,2,128,32]{0,1,2,4,3:T(2,128)(2,1)} %bitcast.114) | data formatting | bytes 1048576 | tf_op jit(solution)/shard_map/all_to_all | solution.py:87
  109.4 0.9 bitcast_multiply_fusion
  110.4 1.5 %slice_bitcast_fusion = (f32[16,1,32,512]{3,2,1,0:T(8,128)}, f32[16,1,32,512]{3,2,1,0:T(8,128)}) fusion(f32[16,32,2,512]{3,1,2,0:T(8,128)S(1)} %bitcast_multiply_fusion), kind=kLoop, calls=%fused_computation.6 | loop fusion | bytes 4194304
  (6 shorter events, 0.1 us)
Async XLA Ops:
  0.6 43.3 %copy-start = (bf16[2,2,8,1,4096]{4,2,3,1,0:T(8,128)(2,1)S(1)}, bf16[2,2,8,1,4096]{4,2,3,1,0:T(8,128)(2,1)}, u32[]{:S(2)}) copy-start(bf16[2,2,8,1,4096]{4,2,3,1,0:T(8,128)(2,1)} %param.7) | copy-start | bytes 786436
  2.2 34.3 %all-to-all-start = ((f32[2,4,128,1]{1,0,3,2:T(2,128)}), f32[2,4,128,1]{1,0,3,2:T(2,128)S(1)}, u32[]{:S(2)}, u32[]{:S(2)}) async-start(f32[2,4,128,1]{1,0,3,2:T(2,128)} %bitcast.4), calls=%async_computation | async-start | bytes 262144 | tf_op jit(solution)/shard_map/all_to_all | solution.py:64
  51.4 22.1 %copy-start.2 = (s32[3,256]{1,0:T(4,128)S(1)}, s32[3,256]{1,0:T(4,128)}, u32[]{:S(2)}) copy-start(s32[3,256]{1,0:T(4,128)} %param.10) | copy-start | bytes 9220
  51.4 22.1 %copy-start.1 = (s32[3,512]{1,0:T(4,128)S(1)}, s32[3,512]{1,0:T(4,128)}, u32[]{:S(2)}) copy-start(s32[3,512]{1,0:T(4,128)} %param.11) | copy-start | bytes 18436
  64.3 32.4 %all-to-all-start.1 = ((bf16[128,2,1024]{2,1,0:T(2,128)(2,1)}), bf16[128,2,1024]{2,1,0:T(2,128)(2,1)S(1)}, u32[]{:S(2)}, u32[]{:S(2)}) async-start(bf16[128,2,1024]{2,1,0:T(2,128)(2,1)} %reshape.658), calls=%async_computation.1 | async-start | bytes 1048576 | tf_op jit(solution)/shard_map/all_to_all | solution.py:87
